TPU v7x, 256 devices: a whole 4x4x8 slice. The times are simulated.
256 devices in a mesh: dp: 16 (over z, x_lo), rep: 4 (over y), ind: 4 (over x_hi, core).
Axes of the slice: x: 4 (x_hi: 2, x_lo: 2; x = x_hi * 2 + x_lo), y: 4, z: 8, core: 2. Of those that a mesh axis runs over, the one named last changes fastest.
Arguments:
- points: bfloat16 [49152, 64], P(('dp', 'rep')), may hold values from -6 to 6
- targets: float32 [49152], P(('dp', 'rep')), may hold values from -6 to 6
- inducing: float32 [4096, 64], P('ind'), may hold values from -6 to 6
- whitening: bfloat16 [4096, 4096], P('ind'), may hold values from -0.01953125 to 0.01953125
- mean_v: float32 [4096], P('ind'), may hold values from -12 to 12
- covariance: float32 [4096, 4096], P('ind', ('dp', 'rep')), may hold values from -24 to 24
- precision: float32 [4096, 4096], P('ind', ('dp', 'rep')), may hold values from -3 to 3
- natural_one: float32 [4096], P('ind'), may hold values from -6 to 6
- lengthscales: float32 [64], replicated, may hold values from 1.6 to 24
- hypers: float32 [2], replicated, may hold values from 0.5 to 2
Outputs:
- precision_new: float32 [4096, 4096], P('ind', ('dp', 'rep'))
- natural_new: float32 [4096], P('ind')
- expected_fit: float32 [], replicated
All inputs are finite; a program needn't handle non-finite values.
Results may differ from a plain program's by a relative error of at most 0.0076.
Values may be sent and summed in bfloat16 or wider, within the bound.
A program may use at most 128 MiB of HBM per device.

v0:
```python
import functools
import jax
import jax.numpy as jnp
from jax import lax
from jax.sharding import Mesh
from jax.sharding import PartitionSpec as P

IND = ("ind_0", "ind_1")
DP_REP = ("dp_0", "dp_1", "rep")
DP_REP_IND = ("dp_0", "dp_1", "rep", "ind_0", "ind_1")


def joined_along(blocks, dim):
    shape = list(blocks.shape[1:])
    shape[dim] *= blocks.shape[0]
    return jnp.moveaxis(blocks, 0, dim).reshape(shape)


def sent_to_all(array, axis):
    copies = jnp.broadcast_to(array, (lax.axis_size(axis), *array.shape))
    return lax.all_to_all(copies, axis, split_axis=0, concat_axis=0, tiled=True)


def collect(array, axis, dim):
    return joined_along(sent_to_all(array, axis), dim)


def of_everyone(array, axis):
    return sent_to_all(array, axis).sum(axis=0)


def together(arrays, axis):
    ends = [0]
    for a in arrays:
        ends.append(ends[-1] + a.size)
    total = of_everyone(jnp.concatenate([a.ravel() for a in arrays]), axis)
    return tuple((total[b:e].reshape(a.shape) for a, b, e in zip(arrays, ends, ends[1:])))


def sum_in_order(blocks, axes, sequence):
    inside = blocks.shape[1:]
    blocks = blocks.reshape(*(lax.axis_size(a) for a in axes), *inside)
    blocks = jnp.moveaxis(blocks, sequence, range(len(axes))).reshape(-1, *inside)
    for k in sequence:
        blocks = lax.psum_scatter(blocks, axes[k], scatter_dimension=0, tiled=True)
    return blocks[0]


def cut_along(array, dim, length):
    before, after = (array.shape[:dim], array.shape[dim + 1 :])
    return jnp.moveaxis(array.reshape(*before, length, -1, *after), dim, 0)


def summed_rows(array, axes, sequence, dim):
    length = lax.axis_size(axes)
    return sum_in_order(cut_along(array, dim, length), axes, sequence)


def one_axis_at_a_time(array, axes):
    return functools.reduce(lax.psum, axes, array)


def cross_cov(inducing, points, lengthscales, signal):
    scaled_z = inducing / lengthscales
    scaled_x = points.astype(jnp.float32) / lengthscales
    norm_z = jnp.sum(scaled_z * scaled_z, axis=1)
    norm_x = jnp.sum(scaled_x * scaled_x, axis=1)
    inner = jnp.dot(scaled_z, scaled_x.T, precision=lax.Precision.HIGHEST)
    return (signal * jnp.exp(-0.5 * (norm_z[:, None] + norm_x[None, :] - 2.0 * inner))).astype(
        jnp.bfloat16
    )


def shards(
    points,
    targets,
    inducing,
    whitening,
    mean_v,
    covariance,
    precision,
    natural_one,
    lengthscales,
    hypers,
):
    signal = hypers[0]
    noise_var = hypers[1]
    all_inducing = collect(inducing, IND, 0)
    cross = cross_cov(all_inducing, points, lengthscales, signal)
    white = jnp.dot(whitening, cross, preferred_element_type=jnp.float32).astype(jnp.bfloat16)
    white_wide = white.astype(jnp.float32)
    mean_part = jnp.dot(mean_v, white_wide, precision=lax.Precision.HIGHEST)
    square_part = jnp.sum(white_wide * white_wide, axis=0)
    gram_part = lax.dot_general(
        white,
        lax.all_gather(white, IND, axis=0, tiled=True),
        (((1,), (1,)), ((), ())),
        preferred_element_type=jnp.float32,
    )
    pred_mean, sq_norm = together((mean_part, square_part), IND)
    resid = targets - pred_mean
    local_fit = jnp.sum(resid * resid + signal - sq_norm)
    local_proj = jnp.dot(white_wide, targets, precision=lax.Precision.HIGHEST)
    proj, fit_sum = together((local_proj, local_fit), DP_REP)
    own_rows = gram_part.shape[0]
    gram = summed_rows(gram_part.astype(jnp.bfloat16), DP_REP, (2, 0, 1), 1).astype(jnp.float32)
    own_cols = gram.shape[1]
    trace = one_axis_at_a_time(jnp.sum(covariance * gram), DP_REP_IND)
    total = points.shape[0] * lax.axis_size(DP_REP)
    expected_fit = -0.5 * jnp.log(2.0 * jnp.pi * noise_var) - (fit_sum + trace) / (
        2.0 * noise_var * total
    )
    row_ids = lax.axis_index(IND) * own_rows + jnp.arange(own_rows, dtype=jnp.int32)
    col_ids = lax.axis_index(DP_REP) * own_cols + jnp.arange(own_cols, dtype=jnp.int32)
    identity = (row_ids[:, None] == col_ids[None, :]).astype(jnp.float32)
    precision_new = 0.5 * precision + 0.5 * (identity + gram / noise_var)
    natural_new = 0.5 * natural_one + 0.5 * proj / noise_var
    return (precision_new, natural_new, expected_fit)


def solution(mesh):
    finer = Mesh(
        mesh.devices.reshape(8, 2, mesh.shape["rep"], 2, 2),
        ("dp_0", "dp_1", "rep", "ind_0", "ind_1"),
    )
    return jax.shard_map(
        shards,
        mesh=finer,
        in_specs=(
            P(DP_REP, None),
            P(DP_REP),
            P(IND, None),
            P(IND, None),
            P(IND),
            P(IND, DP_REP),
            P(IND, DP_REP),
            P(IND),
            P(),
            P(),
        ),
        out_specs=(P(IND, DP_REP), P(IND), P()),
        check_vma=False,
    )
```

profile of v0, /device:TPU:1, one launch (start us, length us, event | category | flops | bytes accessed | tf_op | source)
XLA Modules:
  0.0 345.0 jit_solution(10306386077363218680)
XLA Ops:
  7.2 2.1 broadcast_in_dim.6
  9.3 6.7 %all-to-all-start = ((f32[4,1024,64]{1,2,0:T(8,128)}), f32[4,1024,64]{1,2,0:T(8,128)S(1)}, u32[]{:S(2)}, u32[]{:S(2)}) async-start(f32[4,1024,64]{1,2,0:T(8,128)} %broadcast_in_dim.6), calls=%async_computation | async-start | bytes 2097152 | tf_op jit(solution)/shard_map/all_to_all | solution.py:21
  16.0 1.3 fusion.15
  18.3 12.7 %all-to-all-done = f32[4,1024,64]{1,2,0:T(8,128)S(1)} async-done(((f32[4,1024,64]{1,2,0:T(8,128)}), f32[4,1024,64]{1,2,0:T(8,128)S(1)}, u32[]{:S(2)}, u32[]{:S(2)}) %all-to-all-start) | async-done | bytes 1048608 | tf_op jit(solution)/shard_map/all_to_all | solution.py:21
  32.0 13.6 %multiply_convert_fusion = bf16[4096,768]{1,0:T(8,128)(2,1)S(1)} fusion(f32[768]{0:T(1024)S(1)} %multiply_reduce_fusion.2, f32[4096]{0:T(1024)S(1)} %bitcast.44, f32[]{:T(128)} %bitcast, f32[4096,64]{0,1:T(8,128)S(1)} %bitcast.41, f32[64]{0:T(128)S(1)} %copy-done.7, bf16[768,64]{0,1:T(8,128)(2,1)S(1)} %copy-done.4), kind=kOutput, calls=%fused_computation | convolution fusion | flops 2435153920 | bytes 7458052 | tf_op jit(solution)/shard_map/dot_general | solution.py:68
  45.6 7.9 %multiply_reduce_fusion = (f32[768]{0:T(1024)S(1)}, bf16[768,1024]{1,0:T(8,128)(2,1)}) fusion(bf16[4096,768]{1,0:T(8,128)(2,1)S(1)} %multiply_convert_fusion, bf16[1024,4096]{1,0:T(8,128)(2,1)S(1)} %bitcast.46), kind=kOutput, calls=%fused_computation.2 | convolution fusion | flops 6445595648 | bytes 16256000 | tf_op jit(solution)/shard_map/dot_general | solution.py:90
  53.8 53.3 %all-gather.2.cloned.1.call-done = bf16[4096,768]{0,1:T(8,128)(2,1)} async-done(((bf16[1024,768]{0,1:T(8,128)(2,1)}), bf16[4096,768]{0,1:T(8,128)(2,1)}) %all-gather.2.cloned.1.call-update) | async-done | bytes 6291472 | tf_op jit(solution)/shard_map/all_gather | solution.py:96
  107.1 11.3 %convolution_convert_fusion = bf16[1024,4096]{1,0:T(8,128)(2,1)} fusion(bf16[768,1024]{1,0:T(8,128)(2,1)} %get-tuple-element.8, bf16[4096,768]{0,1:T(8,128)(2,1)} %all-gather.2.cloned.1.call-done), kind=kOutput, calls=%fused_computation.1 | convolution fusion | flops 6446645248 | bytes 16252928 | tf_op jit(solution)/shard_map/dot_general | solution.py:94
  118.4 11.9 %copy.27 = bf16[1024,4096]{0,1:T(8,128)(2,1)} copy(bf16[1024,4096]{1,0:T(8,128)(2,1)} %convolution_convert_fusion) | data formatting | bytes 16777216 | tf_op jit(solution)/shard_map/convert_element_type | solution.py:106
  130.3 8.4 %copy.28 = bf16[4,8,2,1024,64]{3,4,2,1,0:T(8,128)(2,1)} copy(bf16[4,8,2,1024,64]{3,4,0,2,1:T(8,128)(2,1)} %bitcast.38) | data formatting | bytes 16777216 | tf_op jit(solution)/shard_map/transpose | solution.py:43
  138.8 82.2 %reduce-scatter.4.cloned.1.call-done = bf16[16,1024,64]{1,2,0:T(8,128)(2,1)} async-done(((bf16[64,1024,64]{1,2,0:T(8,128)(2,1)}), bf16[16,1024,64]{1,2,0:T(8,128)(2,1)}) %reduce-scatter.4.cloned.1.call-update) | async-done | bytes 2097168 | tf_op jit(solution)/shard_map/reduce_scatter | solution.py:45
  221.1 1.3 convolution_reduce_fusion
  223.1 5.0 %all-to-all-start.1 = ((f32[4,1,1536]{2,1,0:T(1,128)}), f32[4,1,1536]{2,1,0:T(1,128)S(1)}, u32[]{:S(2)}, u32[]{:S(2)}) async-start(f32[4,1,1536]{2,1,0:T(1,128)} %broadcast_in_dim.7), calls=%async_computation.4 | async-start | bytes 49152 | tf_op jit(solution)/shard_map/all_to_all | solution.py:21
  228.1 33.8 %reduce-scatter.6.cloned.1.call-done = bf16[2,1024,64]{1,2,0:T(8,128)(2,1)} async-done(((bf16[16,1024,64]{1,2,0:T(8,128)(2,1)}), bf16[2,1024,64]{1,2,0:T(8,128)(2,1)}) %reduce-scatter.6.cloned.1.call-update) | async-done | bytes 262160 | tf_op jit(solution)/shard_map/reduce_scatter | solution.py:45
  262.7 1.2 fusion.9
  265.5 9.2 %all-to-all-start.2 = ((f32[64,1,1025]{2,1,0:T(1,128)}), f32[64,1,1025]{2,1,0:T(1,128)S(1)}, u32[]{:S(2)}, u32[]{:S(2)}) async-start(f32[64,1,1025]{2,1,0:T(1,128)} %broadcast_in_dim.8), calls=%async_computation.5 | async-start | bytes 589824 | tf_op jit(solution)/shard_map/all_to_all | solution.py:21
  276.0 9.2 %reduce-scatter.8.cloned.1.call-done = bf16[1,1024,64]{1,2,0:T(8,128)(2,1)} async-done(((bf16[2,1024,64]{1,2,0:T(8,128)(2,1)}), bf16[1,1024,64]{1,2,0:T(8,128)(2,1)}) %reduce-scatter.8.cloned.1.call-update) | async-done | bytes 131088 | tf_op jit(solution)/shard_map/reduce_scatter | solution.py:45
  285.2 3.0 fusion.5
  288.2 14.0 %psum.35 = f32[]{:T(128)} all-reduce(f32[]{:T(128)} %get-tuple-element.3), channel_id=1, replica_groups=mesh['dp_0'=8,'dp_1'=2,'rep'=4,'ind_0'=2,'ind_1'=2] {'dp_0'}, use_global_device_ids=true, to_apply=%region_10.0 | all-reduce | flops 1 | bytes 8 | tf_op jit(solution)/shard_map/psum | solution.py:60
  302.2 4.4 %psum.36 = f32[]{:T(128)} all-reduce(f32[]{:T(128)} %psum.35), channel_id=1, replica_groups=mesh['dp_0'=8,'dp_1'=2,'rep'=4,'ind_0'=2,'ind_1'=2] {'dp_1'}, use_global_device_ids=true, to_apply=%region_11.0 | all-reduce | flops 1 | bytes 8 | tf_op jit(solution)/shard_map/psum | solution.py:60
  306.8 9.5 %psum.37 = f32[]{:T(128)} all-reduce(f32[]{:T(128)} %psum.36), channel_id=1, replica_groups=mesh['dp_0'=8,'dp_1'=2,'rep'=4,'ind_0'=2,'ind_1'=2] {'rep'}, use_global_device_ids=true, to_apply=%region_12.0 | all-reduce | flops 1 | bytes 8 | tf_op jit(solution)/shard_map/psum | solution.py:60
  316.4 1.2 fusion.8
  317.6 6.0 %psum.38 = f32[]{:T(128)} all-reduce(f32[]{:T(128)} %psum.37), channel_id=1, replica_groups=mesh['dp_0'=8,'dp_1'=2,'rep'=4,'ind_0'=2,'ind_1'=2] {'ind_0'}, use_global_device_ids=true, to_apply=%region_13.0 | all-reduce | flops 1 | bytes 8 | tf_op jit(solution)/shard_map/psum | solution.py:60
  324.1 11.8 %psum.39 = f32[]{:T(128)} all-reduce(f32[]{:T(128)} %psum.38), channel_id=1, replica_groups=mesh['dp_0'=8,'dp_1'=2,'rep'=4,'ind_0'=2,'ind_1'=2] {'ind_1'}, use_global_device_ids=true, to_apply=%region_14.0 | all-reduce | flops 1 | bytes 8 | tf_op jit(solution)/shard_map/psum | solution.py:60
  (46 shorter events, 6.0 us)
Async XLA Ops:
  7.2 213.9 %copy-start = (f32[1024]{0:T(1024)S(1)}, f32[1024]{0:T(1024)}, u32[]{:S(2)}) copy-start(f32[1024]{0:T(1024)} %param.14) | copy-start | bytes 12292
  7.2 24.7 %copy-start.7 = (f32[64]{0:T(128)S(1)}, f32[64]{0:T(128)}, u32[]{:S(2)}) copy-start(f32[64]{0:T(128)} %param.18) | copy-start | bytes 772
  7.2 24.7 %copy-start.4 = (bf16[768,64]{0,1:T(8,128)(2,1)S(1)}, bf16[768,64]{0,1:T(8,128)(2,1)}, u32[]{:S(2)}) copy-start(bf16[768,64]{0,1:T(8,128)(2,1)} %param.10) | copy-start | bytes 294916
  9.3 21.7 %all-to-all-start = ((f32[4,1024,64]{1,2,0:T(8,128)}), f32[4,1024,64]{1,2,0:T(8,128)S(1)}, u32[]{:S(2)}, u32[]{:S(2)}) async-start(f32[4,1024,64]{1,2,0:T(8,128)} %broadcast_in_dim.6), calls=%async_computation | async-start | bytes 2097152 | tf_op jit(solution)/shard_map/all_to_all | solution.py:21
  16.0 91.1 %all-gather.2.cloned.1.call-start = ((), (), s32[]{:S(2)}) async-start(), calls=%async_computation.6 | async-start | bytes 7864320 | tf_op jit(solution)/shard_map/all_gather | solution.py:96
  31.8 13.7 %slice-start = ((s8[8388608]{0:T(1024)(128)(4,1)}), s8[4194304]{0:T(1024)(128)(4,1)S(1)}, s32[]{:S(2)}) async-start(s8[8388608]{0:T(1024)(128)(4,1)} %bitcast.45), calls=%async_computation.10 | async-start | bytes 8388608
  31.9 13.6 %slice-start.1 = ((s8[8388608]{0:T(1024)(128)(4,1)}), s8[4194304]{0:T(1024)(128)(4,1)S(1)}, s32[]{:S(2)}) async-start(s8[8388608]{0:T(1024)(128)(4,1)} %bitcast.45), calls=%async_computation.11 | async-start | bytes 8388608
  53.6 167.5 %reduce-scatter.4.cloned.1.call-start = ((), (), s32[]{:S(2)}) async-start(), calls=%async_computation.7 | async-start | bytes 10485760 | tf_op jit(solution)/shard_map/reduce_scatter | solution.py:45
  138.7 82.3 %copy-start.5 = (f32[768]{0:T(1024)S(1)}, f32[768]{0:T(1024)}, u32[]{:S(2)}) copy-start(f32[768]{0:T(1024)} %param.11) | copy-start | bytes 9220
  138.7 82.4 %copy-start.1 = (bf16[768,1024]{1,0:T(8,128)(2,1)S(1)}, bf16[768,1024]{1,0:T(8,128)(2,1)}, u32[]{:S(2)}) copy-start(bf16[768,1024]{1,0:T(8,128)(2,1)} %get-tuple-element.8) | copy-start | bytes 4718596
  138.7 146.5 %copy-start.2 = (f32[1024,64]{0,1:T(8,128)S(1)}, f32[1024,64]{0,1:T(8,128)}, u32[]{:S(2)}) copy-start(f32[1024,64]{0,1:T(8,128)} %param.15) | copy-start | bytes 786436
  138.7 146.5 %copy-start.3 = (f32[1024,64]{0,1:T(8,128)S(1)}, f32[1024,64]{0,1:T(8,128)}, u32[]{:S(2)}) copy-start(f32[1024,64]{0,1:T(8,128)} %param.16) | copy-start | bytes 786436
  138.7 177.6 %copy-start.6 = (f32[1024]{0:T(1024)S(1)}, f32[1024]{0:T(1024)}, u32[]{:S(2)}) copy-start(f32[1024]{0:T(1024)} %param.17) | copy-start | bytes 12292
  138.8 123.1 %reduce-scatter.6.cloned.1.call-start = ((), (), s32[]{:S(2)}) async-start(), calls=%async_computation.8 | async-start | bytes 2359296 | tf_op jit(solution)/shard_map/reduce_scatter | solution.py:45
  223.1 39.6 %all-to-all-start.1 = ((f32[4,1,1536]{2,1,0:T(1,128)}), f32[4,1,1536]{2,1,0:T(1,128)S(1)}, u32[]{:S(2)}, u32[]{:S(2)}) async-start(f32[4,1,1536]{2,1,0:T(1,128)} %broadcast_in_dim.7), calls=%async_computation.4 | async-start | bytes 49152 | tf_op jit(solution)/shard_map/all_to_all | solution.py:21
  228.1 57.1 %reduce-scatter.8.cloned.1.call-start = ((), (), s32[]{:S(2)}) async-start(), calls=%async_computation.9 | async-start | bytes 393216 | tf_op jit(solution)/shard_map/reduce_scatter | solution.py:45
  265.5 41.2 %all-to-all-start.2 = ((f32[64,1,1025]{2,1,0:T(1,128)}), f32[64,1,1025]{2,1,0:T(1,128)S(1)}, u32[]{:S(2)}, u32[]{:S(2)}) async-start(f32[64,1,1025]{2,1,0:T(1,128)} %broadcast_in_dim.8), calls=%async_computation.5 | async-start | bytes 589824 | tf_op jit(solution)/shard_map/all_to_all | solution.py:21
Sparse Core Ops, SparseCore 0:
  53.7 53.3 all-gather.1
  138.9 82.1 reduce-scatter.3
  223.6 38.2 reduce-scatter.5
  264.2 20.9 reduce-scatter.7
where the time goes:
time: 346 us; the launch traced here: 345 us
  waiting for transfers between devices  191 us (55%)
  blocking collectives  45.7 us (13%)
  matrix products  34.9 us (10%)
  local copies, waits for them, and re-layouts  25.9 us (7%)
  starting transfers between devices  21.1 us (6%)
  between operations  17.8 us (5%)
  other arithmetic  8.27 us (2%)
    reduce_scatter x3, waiting for transfers between devices, sum_in_order(): blocks = lax.psum_scatter(blocks, axes[k], scatter_dimension=0, tiled=True)  125 us
    all_gather x1, waiting for transfers between devices, shards(): lax.all_gather(white, IND, axis=0, tiled=True)  53.3 us
    psum x5, blocking collectives, one_axis_at_a_time(): return functools.reduce(lax.psum, axes, array)  45.7 us
    all_to_all x3, starting transfers between devices, sent_to_all(): return lax.all_to_all(copies, axis, split_axis=0, concat_axis=0, tiled=True)  20.8 us
    dot_general x1, matrix products, cross_cov(): inner = jnp.dot(scaled_z, scaled_x.T, precision=lax.Precision.HIGHEST)  13.6 us
    all_to_all x3, waiting for transfers between devices, sent_to_all(): return lax.all_to_all(copies, axis, split_axis=0, concat_axis=0, tiled=True)  12.7 us
    convert_element_type x1, local copies, waits for them, and re-layouts, shards(): gram_part.astype(jnp.bfloat16)  11.9 us
    dot_general x1, matrix products, shards(): lax.dot_general(white, lax.all_gather(white, IND, axis=0, tiled=True), ((...  11.3 us
  transfers between devices with their start and end apart: 7, of which 5 were waited for; matrix products, arithmetic and copies ran while one was open for 3% of the time, Pallas kernels for 0%

commit v1 on v0

--- a/solution.py
+++ b/solution.py
@@ -93,7 +93,7 @@
     square_part = jnp.sum(white_wide * white_wide, axis=0)
     gram_part = lax.dot_general(
         white,
-        lax.all_gather(white, IND, axis=0, tiled=True),
+        jnp.concatenate(lax.all_to_all(jnp.stack([white] * lax.axis_size(IND)), IND, 0, 0), axis=0),
         (((1,), (1,)), ((), ())),
         preferred_element_type=jnp.float32,
     )

time: 346 us -> 366 us (1.058)
  blocking collectives: 45.7 us -> 120 us
  waiting for transfers between devices: 191 us -> 139 us
    all_to_all x0 -> x1, blocking collectives: none -> 74.7 us  [shards(): lax.all_to_all(jnp.stack([white] * lax.axis_size(IND)), IND, 0, 0)]
    all_gather x1 -> x0, waiting for transfers between devices: 53.3 us -> none  [shards(): lax.all_gather(white, IND, axis=0, tiled=True)]
  transfers between devices with their start and end apart: 7 -> 6, of which waited for: 5 -> 4; matrix products, arithmetic and copies ran while one was open for 3% -> 3% of each run, Pallas kernels for 0% -> 0%
where the time goes in v1:
time: 366 us; the launch traced here: 365 us
  waiting for transfers between devices  139 us (38%)
  blocking collectives  120 us (33%)
  matrix products  31.5 us (9%)
  local copies, waits for them, and re-layouts  27 us (7%)
  starting transfers between devices  21 us (6%)
  between operations  17.8 us (5%)
  other arithmetic  8.27 us (2%)
    reduce_scatter x3, waiting for transfers between devices, sum_in_order(): blocks = lax.psum_scatter(blocks, axes[k], scatter_dimension=0, tiled=True)  126 us
    all_to_all x1, blocking collectives, shards(): lax.all_to_all(jnp.stack([white] * lax.axis_size(IND)), IND, 0, 0)  74.7 us
    psum x5, blocking collectives, one_axis_at_a_time(): return functools.reduce(lax.psum, axes, array)  45.7 us
    all_to_all x3, starting transfers between devices, sent_to_all(): return lax.all_to_all(copies, axis, split_axis=0, concat_axis=0, tiled=True)  20.7 us
    dot_general x1, matrix products, cross_cov(): inner = jnp.dot(scaled_z, scaled_x.T, precision=lax.Precision.HIGHEST)  13.8 us
    all_to_all x3, waiting for transfers between devices, sent_to_all(): return lax.all_to_all(copies, axis, split_axis=0, concat_axis=0, tiled=True)  12.7 us
    convert_element_type x1, local copies, waits for them, and re-layouts, shards(): gram_part.astype(jnp.bfloat16)  12 us
    dot_general x1, matrix products, shards(): lax.dot_general(white, jnp.concatenate(lax.all_to_all(jnp.stack([white] *...  8.9 us
  transfers between devices with their start and end apart: 6, of which 4 were waited for; matrix products, arithmetic and copies ran while one was open for 3% of the time, Pallas kernels for 0%

profile of v1, /device:TPU:1, one launch (start us, length us, event | category | flops | bytes accessed | tf_op | source)
XLA Modules:
  0.0 365.1 jit_solution(5458592160425357666)
XLA Ops:
  7.2 2.1 broadcast_in_dim.6
  9.3 6.7 %all-to-all-start = ((f32[4,1024,64]{1,2,0:T(8,128)}), f32[4,1024,64]{1,2,0:T(8,128)S(1)}, u32[]{:S(2)}, u32[]{:S(2)}) async-start(f32[4,1024,64]{1,2,0:T(8,128)} %broadcast_in_dim.6), calls=%async_computation | async-start | bytes 2097152 | tf_op jit(solution)/shard_map/all_to_all | solution.py:21
  16.0 1.3 fusion.15
  18.3 12.7 %all-to-all-done = f32[4,1024,64]{1,2,0:T(8,128)S(1)} async-done(((f32[4,1024,64]{1,2,0:T(8,128)}), f32[4,1024,64]{1,2,0:T(8,128)S(1)}, u32[]{:S(2)}, u32[]{:S(2)}) %all-to-all-start) | async-done | bytes 1048608 | tf_op jit(solution)/shard_map/all_to_all | solution.py:21
  32.0 13.8 %multiply_convert_fusion = bf16[4096,768]{1,0:T(8,128)(2,1)S(1)} fusion(f32[768]{0:T(1024)S(1)} %multiply_reduce_fusion.2, f32[4096]{0:T(1024)S(1)} %bitcast.46, f32[]{:T(128)} %bitcast, f32[4096,64]{0,1:T(8,128)S(1)} %bitcast.43, f32[64]{0:T(128)S(1)} %copy-done.6, bf16[768,64]{0,1:T(8,128)(2,1)S(1)} %copy-done.3), kind=kOutput, calls=%fused_computation | convolution fusion | flops 2435153920 | bytes 7458052 | tf_op jit(solution)/shard_map/dot_general | solution.py:68
  45.8 6.8 %multiply_reduce_fusion = (f32[768]{0:T(1024)S(1)}, bf16[768,1024]{1,0:T(8,128)(2,1)S(1)}) fusion(bf16[4096,768]{1,0:T(8,128)(2,1)S(1)} %multiply_convert_fusion, bf16[1024,4096]{1,0:T(8,128)(2,1)S(1)} %bitcast.48), kind=kOutput, calls=%fused_computation.2 | convolution fusion | flops 6445595648 | bytes 16256000 | tf_op jit(solution)/shard_map/dot_general | solution.py:90
  53.7 74.7 %all_to_all.22 = bf16[4,1024,768]{2,1,0:T(8,128)(2,1)S(1)} all-to-all(bf16[4,1024,768]{2,1,0:T(8,128)(2,1)S(1)} %stack.2), channel_id=1, replica_groups=mesh['dp_0'=8,'dp_1'=2,'rep'=4,'ind_0'=2,'ind_1'=2] {'ind_0','ind_1'}, dimensions={0} | all-to-all | bytes 12582912 | tf_op jit(solution)/shard_map/all_to_all | solution.py:96
  128.4 8.9 %convolution_convert_fusion = bf16[1024,4096]{1,0:T(8,128)(2,1)} fusion(bf16[768,1024]{1,0:T(8,128)(2,1)S(1)} %get-tuple-element.8, bf16[4096,768]{1,0:T(8,128)(2,1)S(1)} %bitcast.42), kind=kOutput, calls=%fused_computation.1 | convolution fusion | flops 6446645248 | bytes 16252928 | tf_op jit(solution)/shard_map/dot_general | solution.py:94
  137.3 12.0 %copy.33 = bf16[1024,4096]{0,1:T(8,128)(2,1)} copy(bf16[1024,4096]{1,0:T(8,128)(2,1)} %convolution_convert_fusion) | data formatting | bytes 16777216 | tf_op jit(solution)/shard_map/convert_element_type | solution.py:106
  149.2 8.4 %copy.34 = bf16[4,8,2,1024,64]{3,4,2,1,0:T(8,128)(2,1)} copy(bf16[4,8,2,1024,64]{3,4,0,2,1:T(8,128)(2,1)} %bitcast.39) | data formatting | bytes 16777216 | tf_op jit(solution)/shard_map/transpose | solution.py:43
  157.9 83.0 %reduce-scatter.4.cloned.1.call-done = bf16[16,1024,64]{1,2,0:T(8,128)(2,1)} async-done(((bf16[64,1024,64]{1,2,0:T(8,128)(2,1)}), bf16[16,1024,64]{1,2,0:T(8,128)(2,1)}) %reduce-scatter.4.cloned.1.call-update) | async-done | bytes 2097168 | tf_op jit(solution)/shard_map/reduce_scatter | solution.py:45
  241.0 1.3 convolution_reduce_fusion
  243.0 5.0 %all-to-all-start.2 = ((f32[4,1,1536]{2,1,0:T(1,128)}), f32[4,1,1536]{2,1,0:T(1,128)S(1)}, u32[]{:S(2)}, u32[]{:S(2)}) async-start(f32[4,1,1536]{2,1,0:T(1,128)} %broadcast_in_dim.7), calls=%async_computation.5 | async-start | bytes 49152 | tf_op jit(solution)/shard_map/all_to_all | solution.py:21
  248.0 33.9 %reduce-scatter.6.cloned.1.call-done = bf16[2,1024,64]{1,2,0:T(8,128)(2,1)} async-done(((bf16[16,1024,64]{1,2,0:T(8,128)(2,1)}), bf16[2,1024,64]{1,2,0:T(8,128)(2,1)}) %reduce-scatter.6.cloned.1.call-update) | async-done | bytes 262160 | tf_op jit(solution)/shard_map/reduce_scatter | solution.py:45
  282.7 1.2 fusion.9
  285.4 9.1 %all-to-all-start.3 = ((f32[64,1,1025]{2,1,0:T(1,128)}), f32[64,1,1025]{2,1,0:T(1,128)S(1)}, u32[]{:S(2)}, u32[]{:S(2)}) async-start(f32[64,1,1025]{2,1,0:T(1,128)} %broadcast_in_dim.8), calls=%async_computation.6 | async-start | bytes 589824 | tf_op jit(solution)/shard_map/all_to_all | solution.py:21
  295.9 9.5 %reduce-scatter.8.cloned.1.call-done = bf16[1,1024,64]{1,2,0:T(8,128)(2,1)} async-done(((bf16[2,1024,64]{1,2,0:T(8,128)(2,1)}), bf16[1,1024,64]{1,2,0:T(8,128)(2,1)}) %reduce-scatter.8.cloned.1.call-update) | async-done | bytes 131088 | tf_op jit(solution)/shard_map/reduce_scatter | solution.py:45
  305.4 3.0 fusion.5
  308.4 14.2 %psum.35 = f32[]{:T(128)} all-reduce(f32[]{:T(128)} %get-tuple-element.3), channel_id=1, replica_groups=mesh['dp_0'=8,'dp_1'=2,'rep'=4,'ind_0'=2,'ind_1'=2] {'dp_0'}, use_global_device_ids=true, to_apply=%region_10.0 | all-reduce | flops 1 | bytes 8 | tf_op jit(solution)/shard_map/psum | solution.py:60
  322.6 4.4 %psum.36 = f32[]{:T(128)} all-reduce(f32[]{:T(128)} %psum.35), channel_id=1, replica_groups=mesh['dp_0'=8,'dp_1'=2,'rep'=4,'ind_0'=2,'ind_1'=2] {'dp_1'}, use_global_device_ids=true, to_apply=%region_11.0 | all-reduce | flops 1 | bytes 8 | tf_op jit(solution)/shard_map/psum | solution.py:60
  327.2 9.2 %psum.37 = f32[]{:T(128)} all-reduce(f32[]{:T(128)} %psum.36), channel_id=1, replica_groups=mesh['dp_0'=8,'dp_1'=2,'rep'=4,'ind_0'=2,'ind_1'=2] {'rep'}, use_global_device_ids=true, to_apply=%region_12.0 | all-reduce | flops 1 | bytes 8 | tf_op jit(solution)/shard_map/psum | solution.py:60
  336.4 1.2 fusion.8
  337.6 6.0 %psum.38 = f32[]{:T(128)} all-reduce(f32[]{:T(128)} %psum.37), channel_id=1, replica_groups=mesh['dp_0'=8,'dp_1'=2,'rep'=4,'ind_0'=2,'ind_1'=2] {'ind_0'}, use_global_device_ids=true, to_apply=%region_13.0 | all-reduce | flops 1 | bytes 8 | tf_op jit(solution)/shard_map/psum | solution.py:60
  344.1 11.9 %psum.39 = f32[]{:T(128)} all-reduce(f32[]{:T(128)} %psum.38), channel_id=1, replica_groups=mesh['dp_0'=8,'dp_1'=2,'rep'=4,'ind_0'=2,'ind_1'=2] {'ind_1'}, use_global_device_ids=true, to_apply=%region_14.0 | all-reduce | flops 1 | bytes 8 | tf_op jit(solution)/shard_map/psum | solution.py:60
  (44 shorter events, 7.1 us)
Async XLA Ops:
  7.2 233.9 %copy-start = (f32[1024]{0:T(1024)S(1)}, f32[1024]{0:T(1024)}, u32[]{:S(2)}) copy-start(f32[1024]{0:T(1024)} %param.14) | copy-start | bytes 12292
  7.2 24.7 %copy-start.6 = (f32[64]{0:T(128)S(1)}, f32[64]{0:T(128)}, u32[]{:S(2)}) copy-start(f32[64]{0:T(128)} %param.18) | copy-start | bytes 772
  7.2 24.7 %copy-start.3 = (bf16[768,64]{0,1:T(8,128)(2,1)S(1)}, bf16[768,64]{0,1:T(8,128)(2,1)}, u32[]{:S(2)}) copy-start(bf16[768,64]{0,1:T(8,128)(2,1)} %param.10) | copy-start | bytes 294916
  9.3 21.7 %all-to-all-start = ((f32[4,1024,64]{1,2,0:T(8,128)}), f32[4,1024,64]{1,2,0:T(8,128)S(1)}, u32[]{:S(2)}, u32[]{:S(2)}) async-start(f32[4,1024,64]{1,2,0:T(8,128)} %broadcast_in_dim.6), calls=%async_computation | async-start | bytes 2097152 | tf_op jit(solution)/shard_map/all_to_all | solution.py:21
  16.0 225.0 %reduce-scatter.4.cloned.1.call-start = ((), (), s32[]{:S(2)}) async-start(), calls=%async_computation.7 | async-start | bytes 10485760 | tf_op jit(solution)/shard_map/reduce_scatter | solution.py:45
  31.8 13.9 %slice-start = ((s8[8388608]{0:T(1024)(128)(4,1)}), s8[4194304]{0:T(1024)(128)(4,1)S(1)}, s32[]{:S(2)}) async-start(s8[8388608]{0:T(1024)(128)(4,1)} %bitcast.47), calls=%async_computation.10 | async-start | bytes 8388608
  31.9 13.8 %slice-start.1 = ((s8[8388608]{0:T(1024)(128)(4,1)}), s8[4194304]{0:T(1024)(128)(4,1)S(1)}, s32[]{:S(2)}) async-start(s8[8388608]{0:T(1024)(128)(4,1)} %bitcast.47), calls=%async_computation.11 | async-start | bytes 8388608
  157.6 83.4 %copy-start.4 = (f32[768]{0:T(1024)S(1)}, f32[768]{0:T(1024)}, u32[]{:S(2)}) copy-start(f32[768]{0:T(1024)} %param.11) | copy-start | bytes 9220
  157.6 147.8 %copy-start.1 = (f32[1024,64]{0,1:T(8,128)S(1)}, f32[1024,64]{0,1:T(8,128)}, u32[]{:S(2)}) copy-start(f32[1024,64]{0,1:T(8,128)} %param.15) | copy-start | bytes 786436
  157.6 147.8 %copy-start.2 = (f32[1024,64]{0,1:T(8,128)S(1)}, f32[1024,64]{0,1:T(8,128)}, u32[]{:S(2)}) copy-start(f32[1024,64]{0,1:T(8,128)} %param.16) | copy-start | bytes 786436
  157.6 178.8 %copy-start.5 = (f32[1024]{0:T(1024)S(1)}, f32[1024]{0:T(1024)}, u32[]{:S(2)}) copy-start(f32[1024]{0:T(1024)} %param.17) | copy-start | bytes 12292
  157.7 124.2 %reduce-scatter.6.cloned.1.call-start = ((), (), s32[]{:S(2)}) async-start(), calls=%async_computation.8 | async-start | bytes 2359296 | tf_op jit(solution)/shard_map/reduce_scatter | solution.py:45
  243.0 39.6 %all-to-all-start.2 = ((f32[4,1,1536]{2,1,0:T(1,128)}), f32[4,1,1536]{2,1,0:T(1,128)S(1)}, u32[]{:S(2)}, u32[]{:S(2)}) async-start(f32[4,1,1536]{2,1,0:T(1,128)} %broadcast_in_dim.7), calls=%async_computation.5 | async-start | bytes 49152 | tf_op jit(solution)/shard_map/all_to_all | solution.py:21
  248.0 57.4 %reduce-scatter.8.cloned.1.call-start = ((), (), s32[]{:S(2)}) async-start(), calls=%async_computation.9 | async-start | bytes 393216 | tf_op jit(solution)/shard_map/reduce_scatter | solution.py:45
  285.4 41.6 %all-to-all-start.3 = ((f32[64,1,1025]{2,1,0:T(1,128)}), f32[64,1,1025]{2,1,0:T(1,128)S(1)}, u32[]{:S(2)}, u32[]{:S(2)}) async-start(f32[64,1,1025]{2,1,0:T(1,128)} %broadcast_in_dim.8), calls=%async_computation.6 | async-start | bytes 589824 | tf_op jit(solution)/shard_map/all_to_all | solution.py:21
Sparse Core Ops, SparseCore 0:
  157.8 83.1 reduce-scatter.3
  243.5 38.3 reduce-scatter.5
  284.4 20.9 reduce-scatter.7
